TPU v7x, 32 devices: a whole 2x2x4 slice. The times are simulated.
32 devices in a mesh: stn: 4 (over z), chan: 4 (over y, core), tile: 2 (over x).
Axes of the slice: x: 2, y: 2, z: 4, core: 2. Of those that a mesh axis runs over, the one named last changes fastest.
Arguments:
- model_image: bfloat16 [8, 64, 2048], P('tile', 'stn'), may hold values from -0.005859375 to 0.005859375
- station_beams: float32 [2, 64, 1024], replicated, may hold values from -6 to 6
- subgrid_offsets: int32 [4, 128, 2], P('chan'), may hold values from -4096 to 4064
- subgrid_stations: int32 [128, 2], P(('stn', 'tile')), may hold values from 0 to 63, as said below
- visibility_uv: float32 [2, 128, 512], P(None, ('stn', 'tile'), 'chan'), may hold values from 2 to 30
- observed: float32 [2, 32, 4, 512], P(None, ('stn', 'tile'), 'chan'), may hold values from -3 to 3
- live_counts: int32 [32, 4], P(('stn', 'tile'), 'chan'), may hold values from 1 to 8
Outputs:
- residual: float32 [2, 32, 4, 512], P(None, ('stn', 'tile'), 'chan')
Inputs may be any that keep to these rules, and one draw needn't show every extreme that they name: `subgrid_stations`: each row names two different stations. `live_counts`: rows with a time step at or beyond the count carry no data.
All inputs are finite; a program needn't handle non-finite values.
Results may differ from a plain program's by a relative error of at most 0.00071.
Values may be sent and summed in bfloat16 or wider, within the bound.
A program may use at most 64 MiB of HBM per device.

v0:
```python
import math
import jax
import jax.numpy as jnp
from jax import lax
from jax.sharding import PartitionSpec as P

SG = 32
NG = 8192
TIMES = 8
TILE_DEV = 4
TL = 64
SUB_TILE = 16
two_pi = 6.283185307179586


def phase_pair(products, modulus):
    angle_turns = jnp.mod(products, modulus).astype(jnp.float32) * (two_pi / modulus)
    return (jnp.cos(angle_turns), -jnp.sin(angle_turns))


def narrow_mix(pattern, left, right):
    return jnp.einsum(pattern, left, right, preferred_element_type=jnp.float32)


def exact_mix(pattern, left, right):
    return jnp.einsum(pattern, left, right, precision=lax.Precision.HIGHEST)


def tile_cuts(strip_rows, row_ids, offset_block, strip_half):
    block_size = offset_block.shape[0]
    columns = strip_rows.shape[1]
    pixel_idx = jnp.arange(SG, dtype=jnp.int32)
    col_pos = jnp.arange(columns, dtype=jnp.int32) - columns // 2
    v_index = offset_block[:, 1][:, None] + pixel_idx[None, :]
    ev_real, ev_imag = phase_pair(col_pos[:, None, None] * v_index[None, :, :], NG)
    phase_table = (
        jnp.stack([ev_real, ev_imag], axis=1)
        .reshape(columns, 2 * block_size * SG)
        .astype(jnp.bfloat16)
    )
    partial_q = jnp.dot(strip_rows, phase_table, preferred_element_type=jnp.float32).astype(
        jnp.bfloat16
    )
    partial_q = partial_q.reshape(strip_rows.shape[0], 2, block_size, SG)
    q_real = partial_q[:, 0]
    q_imag = partial_q[:, 1]
    u_index = offset_block[:, 0][:, None] + pixel_idx[None, :]
    row_pos = row_ids - strip_half
    eu_real, eu_imag = phase_pair(u_index[:, :, None] * row_pos[None, None, :], NG)
    eu_real = eu_real.astype(jnp.bfloat16)
    eu_imag = eu_imag.astype(jnp.bfloat16)
    cut_real = narrow_mix("jal,ljb->jab", eu_real, q_real) - narrow_mix(
        "jal,ljb->jab", eu_imag, q_imag
    )
    cut_imag = narrow_mix("jal,ljb->jab", eu_real, q_imag) + narrow_mix(
        "jal,ljb->jab", eu_imag, q_real
    )
    return jnp.stack([cut_real, cut_imag], axis=1).reshape(block_size, 2 * SG * SG)


def cuts_blocked(strip_rows, row_ids, offsets, strip_half):
    how_many = offsets.shape[0]
    block_size = math.gcd(how_many, 32)
    grouped = offsets.reshape(how_many // block_size, block_size, 2)
    stacked = lax.map(
        lambda offset_block: tile_cuts(strip_rows, row_ids, offset_block, strip_half), grouped
    )
    return stacked.reshape(how_many, 2 * SG * SG)


def predict(cut_rows, pair_ids, station_beams, uv_block):
    how_many = cut_rows.shape[0]
    cut_grid = cut_rows.reshape(how_many, 2, SG, SG)
    pixel_idx = jnp.arange(SG, dtype=jnp.int32)
    w_real, w_neg = phase_pair(pixel_idx[:, None] * pixel_idx[None, :], SG)
    w_imag = -w_neg
    c_real = cut_grid[:, 0]
    c_imag = cut_grid[:, 1]
    half_real = exact_mix("xa,jab->jxb", w_real, c_real) - exact_mix("xa,jab->jxb", w_imag, c_imag)
    half_imag = exact_mix("xa,jab->jxb", w_real, c_imag) + exact_mix("xa,jab->jxb", w_imag, c_real)
    sub_real = (
        exact_mix("jxb,yb->jxy", half_real, w_real) - exact_mix("jxb,yb->jxy", half_imag, w_imag)
    ) / (SG * SG)
    sub_imag = (
        exact_mix("jxb,yb->jxy", half_real, w_imag) + exact_mix("jxb,yb->jxy", half_imag, w_real)
    ) / (SG * SG)
    pixel_pos = pixel_idx.astype(jnp.float32)
    taper_line = 1.0 - ((2.0 * pixel_pos - (SG - 1)) / SG) ** 2
    taper_grid = (taper_line[:, None] * taper_line[None, :]).reshape(SG * SG)
    beam_first = station_beams[:, pair_ids[:, 0]]
    beam_second = station_beams[:, pair_ids[:, 1]]
    gain_real = (beam_first[0] * beam_second[0] + beam_first[1] * beam_second[1]) * taper_grid
    gain_imag = (beam_first[1] * beam_second[0] - beam_first[0] * beam_second[1]) * taper_grid
    flat_real = sub_real.reshape(how_many, SG * SG)
    flat_imag = sub_imag.reshape(how_many, SG * SG)
    weighted_real = (flat_real * gain_real - flat_imag * gain_imag).reshape(how_many, SG, SG)
    weighted_imag = (flat_real * gain_imag + flat_imag * gain_real).reshape(how_many, SG, SG)
    u_angle = uv_block[0][:, :, None] * pixel_pos[None, None, :] * (two_pi / SG)
    v_angle = uv_block[1][:, :, None] * pixel_pos[None, None, :] * (two_pi / SG)
    eu_real = jnp.cos(u_angle)
    eu_imag = -jnp.sin(u_angle)
    ev_real = jnp.cos(v_angle)
    ev_imag = -jnp.sin(v_angle)
    inner_real = exact_mix("jxy,jky->jxk", weighted_real, ev_real) - exact_mix(
        "jxy,jky->jxk", weighted_imag, ev_imag
    )
    inner_imag = exact_mix("jxy,jky->jxk", weighted_real, ev_imag) + exact_mix(
        "jxy,jky->jxk", weighted_imag, ev_real
    )
    vis_real = exact_mix("jkx,jxk->jk", eu_real, inner_real) - exact_mix(
        "jkx,jxk->jk", eu_imag, inner_imag
    )
    vis_imag = exact_mix("jkx,jxk->jk", eu_real, inner_imag) + exact_mix(
        "jkx,jxk->jk", eu_imag, inner_real
    )
    return jnp.stack([vis_real, vis_imag], axis=0)


def on_device(
    model_image,
    station_beams,
    subgrid_offsets,
    subgrid_stations,
    visibility_uv,
    observed,
    live_counts,
):
    tile_count = lax.axis_size("tile")
    columns = model_image.shape[2]
    strip_half = TILE_DEV * tile_count * TL // 2
    group_offsets = subgrid_offsets[0]
    stn_index = lax.axis_index("stn")
    tile_first = lax.axis_index("tile") * TILE_DEV
    tile_ids = jnp.arange(TILE_DEV, dtype=jnp.int32)
    group_size = SUB_TILE * tile_count
    station_offsets = lax.dynamic_slice_in_dim(group_offsets, stn_index * group_size, group_size, 0)
    shard_piece = lax.all_gather(model_image, "stn", axis=1, tiled=True)
    piece_rows = shard_piece.shape[1]
    piece_ids = (
        (tile_first + tile_ids)[:, None] * TL + jnp.arange(piece_rows, dtype=jnp.int32)[None, :]
    ).reshape(-1)
    piece_strip = shard_piece.reshape(TILE_DEV * piece_rows, columns)
    group_cuts = cuts_blocked(piece_strip, piece_ids, station_offsets, strip_half)
    own_cuts = lax.psum_scatter(group_cuts, "tile", scatter_dimension=0, tiled=True)
    predicted = predict(own_cuts, subgrid_stations, station_beams, visibility_uv)
    chan_count = lax.axis_size("chan")
    outgoing = predicted.reshape(2, SUB_TILE // chan_count, chan_count, predicted.shape[2])
    regrouped = lax.all_to_all(outgoing, "chan", split_axis=2, concat_axis=3, tiled=True)
    total_rows = regrouped.shape[3]
    time_step = jnp.mod(jnp.arange(total_rows, dtype=jnp.int32), TIMES)
    live_mask = time_step[None, None, :] < live_counts[:, :, None]
    return jnp.where(live_mask[None], observed - regrouped, 0.0)


def solution(mesh):
    return jax.shard_map(
        on_device,
        mesh=mesh,
        in_specs=(
            P("tile", "stn", None),
            P(),
            P("chan", None, None),
            P(("stn", "tile"), None),
            P(None, ("stn", "tile"), "chan"),
            P(None, ("stn", "tile"), "chan", None),
            P(("stn", "tile"), "chan"),
        ),
        out_specs=P(None, ("stn", "tile"), "chan", None),
        check_vma=False,
    )
```

profile of v0, /device:TPU:0, one launch (start us, length us, event | category | flops | bytes accessed | tf_op | source)
XLA Modules:
  0.0 118.8 jit_solution(3581766435553474679)
XLA Ops:
  6.5 0.7 all-gather.2.cloned.1.call-update
  7.3 0.8 dynamic-slice_bitcast_fusion
  8.3 0.8 fusion.66
  9.1 0.7 gather_fusion
  9.9 0.7 gather_fusion.1
  10.8 0.1 sub.77
  11.0 35.5 %cosine_convert_fusion = (bf16[2048,1,32,32]{0,3,2,1:T(8,128)(2,1)S(1)}, bf16[2048,1,32,32]{0,3,2,1:T(8,128)(2,1)}) fusion(s32[32,32]{1,0:T(8,128)S(1)} %iota_add_fusion, s32[2048]{0:T(1024)S(1)} %iota_add_fusion.2), kind=kLoop, calls=%fused_computation.12 | loop fusion | flops 35651584 | bytes 8400896 | tf_op jit(solution)/shard_map/convert
  46.4 6.2 %pad_maximum_fusion = bf16[2048,2,32,32]{0,3,2,1:T(8,128)(2,1)} fusion(bf16[2048,1,32,32]{0,3,2,1:T(8,128)(2,1)} %get-tuple-element.31, bf16[2048,1,32,32]{0,3,2,1:T(8,128)(2,1)S(1)} %get-tuple-element.30), kind=kLoop, calls=%fused_computation.10 | loop fusion | flops 4194304 | bytes 16777216 | tf_op jit(solution)/shard_map/while/body/eval_jaxpr/stack | solution.py:37
  52.6 6.0 %convolution_convert_fusion = bf16[2048,256]{1,0:T(8,128)(2,1)S(1)} fusion(bf16[2048,2048]{0,1:T(8,128)(2,1)} %bitcast.90, bf16[256,2048]{1,0:T(8,128)(2,1)} %bitcast.96), kind=kOutput, calls=%fused_computation.13 | convolution fusion | flops 2148007936 | bytes 10485760 | tf_op jit(solution)/shard_map/while/body/eval_jaxpr/dot_general | solution.py:41
  58.6 4.0 %fusion.15 = f32[32,32,32]{2,1,0:T(8,128)S(1)} fusion(s32[256]{0:T(256)S(1)} %sub.67, s32[32,32]{1,0:T(8,128)S(1)} %iota_add_fusion.1, bf16[256,2,32,32]{0,3,2,1:T(8,128)(2,1)S(1)} %bitcast.97), kind=kOutput, calls=%fused_computation.44 | convolution fusion | flops 20709376 | bytes 672768 | tf_op jit(solution)/shard_map/while/body/eval_jaxpr/jal,ljb->jab/dot_general | solution.py:22
  62.6 4.0 %fusion.14 = f32[32,32,32]{2,1,0:T(8,128)S(1)} fusion(s32[256]{0:T(256)S(1)} %sub.67, s32[32,32]{1,0:T(8,128)S(1)} %iota_add_fusion.1, bf16[256,2,32,32]{0,3,2,1:T(8,128)(2,1)S(1)} %bitcast.98), kind=kOutput, calls=%fused_computation.43 | convolution fusion | flops 20709376 | bytes 672768 | tf_op jit(solution)/shard_map/while/body/eval_jaxpr/jal,ljb->jab/dot_general | solution.py:22
  66.6 4.3 %fusion.4 = f32[32,1,32,32]{3,2,0,1:T(8,128)S(1)} fusion(f32[32,32,32]{2,1,0:T(8,128)S(1)} %fusion.15, s32[256]{0:T(256)S(1)} %sub.67, s32[32,32]{1,0:T(8,128)S(1)} %iota_add_fusion.1, bf16[256,2,32,32]{0,3,2,1:T(8,128)(2,1)S(1)} %bitcast.99), kind=kOutput, calls=%fused_computation.22 | convolution fusion | flops 21004288 | bytes 1197056 | tf_op jit(solution)/shard_map/while/body/eval_jaxpr/jal,ljb->jab/dot_general | solution.py:22
  70.9 4.1 %fusion.3 = f32[32,1,32,32]{3,2,0,1:T(8,128)S(1)} fusion(f32[32,32,32]{2,1,0:T(8,128)S(1)} %fusion.14, s32[256]{0:T(256)S(1)} %sub.67, s32[32,32]{1,0:T(8,128)S(1)} %iota_add_fusion.1, bf16[256,2,32,32]{0,3,2,1:T(8,128)(2,1)S(1)} %bitcast.100), kind=kOutput, calls=%fused_computation.20 | convolution fusion | flops 21004288 | bytes 1197056 | tf_op jit(solution)/shard_map/while/body/eval_jaxpr/jal,ljb->jab/dot_general | solution.py:22
  75.2 1.2 %reshape.278 = f32[32,2048]{1,0:T(8,128)} reshape(f32[32,2,32,32]{3,2,1,0:T(8,128)S(1)} %copy.26) | data formatting | bytes 524288 | tf_op jit(solution)/shard_map/reshape | solution.py:68
  76.5 14.6 %reduce-scatter.2.cloned.1.call-done = f32[16,2048]{1,0:T(8,128)} async-done(((f32[32,2048]{1,0:T(8,128)}), f32[16,2048]{1,0:T(8,128)}) %reduce-scatter.2.cloned.1.call-update) | async-done | bytes 131088 | tf_op jit(solution)/shard_map/reduce_scatter | solution.py:144
  91.1 1.1 reshape.279
  92.2 0.6 fusion.23
  92.8 0.6 fusion.22
  93.4 0.6 fusion.10
  94.0 0.6 fusion.46
  94.6 0.6 fusion.39
  95.2 0.6 fusion.9
  95.8 0.9 fusion.8
  96.6 0.6 multiply_add_fusion
  97.2 1.3 %fusion.18 = f32[16,32,128]{2,1,0:T(8,128)S(1)} fusion(f32[16,32,32]{2,1,0:T(8,128)S(1)} %get-tuple-element.27, f32[16,128]{1,0:T(8,128)S(1)} %get-tuple-element.33, f32[32]{0:T(128)S(1)} %iota_convert_fusion), kind=kOutput, calls=%fused_computation.56 | convolution fusion | flops 25296896 | bytes 336000 | tf_op jit(solution)/shard_map/jxy,jky->jxk/dot_general | solution.py:26
  98.6 1.3 %fusion.20 = f32[16,32,128]{2,1,0:T(8,128)S(1)} fusion(f32[16,32,32]{2,1,0:T(8,128)S(1)} %get-tuple-element.27, f32[16,128]{1,0:T(8,128)S(1)} %get-tuple-element.33, f32[32]{0:T(128)S(1)} %iota_convert_fusion), kind=kOutput, calls=%fused_computation.57 | convolution fusion | flops 25362432 | bytes 336000 | tf_op jit(solution)/shard_map/jxy,jky->jxk/dot_general | solution.py:26
  99.9 1.3 %fusion.6 = f32[16,128,32]{1,2,0:T(8,128)S(1)} fusion(f32[16,32,128]{2,1,0:T(8,128)S(1)} %fusion.18, f32[16,32,32]{2,1,0:T(8,128)S(1)} %get-tuple-element.26, f32[16,128]{1,0:T(8,128)S(1)} %get-tuple-element.33, f32[32]{0:T(128)S(1)} %iota_convert_fusion), kind=kOutput, calls=%fused_computation.26 | convolution fusion | flops 25427968 | bytes 598144 | tf_op jit(solution)/shard_map/jxy,jky->jxk/dot_general | solution.py:26
  101.2 2.4 %multiply_reduce_fusion.2 = (f32[16,128]{1,0:T(8,128)S(1)}, f32[16,128]{1,0:T(8,128)S(1)}, f32[16,128]{1,0:T(8,128)S(1)}, f32[16,128]{1,0:T(8,128)S(1)}) fusion(f32[32]{0:T(128)S(1)} %iota_convert_fusion, f32[16,128]{1,0:T(8,128)S(1)} %get-tuple-element.32, f32[16,128,32]{1,2,0:T(8,128)S(1)} %fusion.6, f32[16,32,128]{2,1,0:T(8,128)S(1)} %fusion.20, ...), kind=kOutput, calls=%fused_computation.49 | convolution fusion | flops 26075136 | bytes 639104 | tf_op jit(solution)/shard_map/jxy,jky->jxk/dot_general | solution.py:26
  103.6 0.6 copy.33
  104.2 3.3 %all-to-all-start = ((f32[2,4,4,128]{3,1,0,2:T(4,128)}), f32[2,4,4,128]{3,1,0,2:T(4,128)S(1)}, u32[]{:S(2)}, u32[]{:S(2)}) async-start(f32[2,4,4,128]{3,1,0,2:T(4,128)} %copy.33), calls=%async_computation.1 | async-start | bytes 32768 | tf_op jit(solution)/shard_map/all_to_all | solution.py:148
  107.6 3.7 %all-to-all-done = f32[2,4,4,128]{3,1,0,2:T(4,128)S(1)} async-done(((f32[2,4,4,128]{3,1,0,2:T(4,128)}), f32[2,4,4,128]{3,1,0,2:T(4,128)S(1)}, u32[]{:S(2)}, u32[]{:S(2)}) %all-to-all-start) | async-done | bytes 16416 | tf_op jit(solution)/shard_map/all_to_all | solution.py:148
  111.4 0.6 copy.36
  (36 shorter events, 0.9 us)
Async XLA Ops:
  6.5 2.6 %copy-start = (f32[2,64,1024]{2,1,0:T(8,128)S(1)}, f32[2,64,1024]{2,1,0:T(8,128)}, u32[]{:S(2)}) copy-start(f32[2,64,1024]{2,1,0:T(8,128)} %param.8) | copy-start | bytes 1572868
  6.5 46.1 %all-gather.2.cloned.1.call-start = ((), (), s32[]{:S(2)}) async-start(), calls=%async_computation.2 | async-start | bytes 1310720 | tf_op jit(solution)/shard_map/all_gather | solution.py:137
  7.3 83.8 %reduce-scatter.2.cloned.1.call-start = ((), (), s32[]{:S(2)}) async-start(), calls=%async_computation.3 | async-start | bytes 393216 | tf_op jit(solution)/shard_map/reduce_scatter | solution.py:144
  66.6 9.9 %copy-start.2 = (f32[2,16,128]{2,1,0:T(8,128)S(1)}, f32[2,16,128]{2,1,0:T(8,128)}, u32[]{:S(2)}) copy-start(f32[2,16,128]{2,1,0:T(8,128)} %param.11) | copy-start | bytes 49156
  75.0 32.5 %copy-start.3 = (s32[4,1]{0,1:T(1,128)S(1)}, s32[4,1]{0,1:T(1,128)}, u32[]{:S(2)}) copy-start(s32[4,1]{0,1:T(1,128)} %param.13) | copy-start | bytes 52
  75.0 36.3 %copy-start.1 = (f32[2,4,1,512]{3,2,1,0:T(1,128)S(1)}, f32[2,4,1,512]{3,2,1,0:T(1,128)}, u32[]{:S(2)}) copy-start(f32[2,4,1,512]{3,2,1,0:T(1,128)} %param.12) | copy-start | bytes 49156
  104.2 7.1 %all-to-all-start = ((f32[2,4,4,128]{3,1,0,2:T(4,128)}), f32[2,4,4,128]{3,1,0,2:T(4,128)S(1)}, u32[]{:S(2)}, u32[]{:S(2)}) async-start(f32[2,4,4,128]{3,1,0,2:T(4,128)} %copy.33), calls=%async_computation.1 | async-start | bytes 32768 | tf_op jit(solution)/shard_map/all_to_all | solution.py:148
Sparse Core Ops, SparseCore 0:
  8.9 30.7 all-gather.1
  76.6 14.4 reduce-scatter.1
where the time goes:
time: 119 us
  other arithmetic  43 us (36%)
  matrix products  33.7 us (28%)
  waiting for transfers between devices  19 us (16%)
  between operations  13.6 us (11%)
  local copies, waits for them, and re-layouts  6.18 us (5%)
  starting transfers between devices  3.3 us (3%)
    another operation x1, other arithmetic  35.5 us
    dot_general x4, matrix products, narrow_mix(): return jnp.einsum(pattern, left, right, preferred_element_type=jnp.float32)  16.4 us
    reduce_scatter x1, waiting for transfers between devices, on_device(): lax.psum_scatter(group_cuts, 'tile', scatter_dimension=0, tiled=True)  14.6 us
    dot_general x12, matrix products, exact_mix(): return jnp.einsum(pattern, left, right, precision=lax.Precision.HIGHEST)  11.3 us
    another operation x1, other arithmetic, tile_cuts(): jnp.stack([ev_real, ev_imag], axis=1).reshape(columns, 2 * block_size * SG)  6.18 us
    dot_general x1, matrix products, tile_cuts(): jnp.dot(strip_rows, phase_table, preferred_element_type=jnp.float32)  6 us
    all_to_all x1, waiting for transfers between devices, on_device(): lax.all_to_all(outgoing, 'chan', split_axis=2, concat_axis=3, tiled=True)  3.74 us
    all_to_all x1, starting transfers between devices, on_device(): lax.all_to_all(outgoing, 'chan', split_axis=2, concat_axis=3, tiled=True)  3.25 us
  transfers between devices with their start and end apart: 3, of which 2 were waited for; matrix products, arithmetic and copies ran while one was open for 38% of the time, Pallas kernels for 0%

commit v1 on v0

--- a/solution.py
+++ b/solution.py
@@ -1,3 +1,4 @@
+import functools
 import math
 import jax
 import jax.numpy as jnp
@@ -11,6 +12,42 @@
 TL = 64
 SUB_TILE = 16
 two_pi = 6.283185307179586
+
+
+def name_plate_on(field_in, k_dim, buf):
+    f_now = field_in.shape
+    e_now = jnp.moveaxis(
+        field_in.reshape(*f_now[:k_dim], buf, f_now[k_dim] // buf, *f_now[k_dim + 1 :]), k_dim, 0
+    )
+    return e_now
+
+
+def reach_meshes_all(chunk, on_dim):
+    all_rows = list(chunk.shape[1:])
+    all_rows[on_dim] *= chunk.shape[0]
+    step_out = jnp.moveaxis(chunk, 0, on_dim).reshape(all_rows)
+    return step_out
+
+
+def plan_racks_on(target, vector, row_axis, message):
+    state_now, u_next = (jax.lax.psum(1, axis_name=row_axis), jax.lax.axis_index(row_axis))
+    current_arr = name_plate_on(target, message, state_now)
+    rr = 1
+    runs = [current_arr[u_next]]
+    while rr < state_now:
+        latest = current_arr[u_next ^ rr]
+        runs.append(
+            jax.lax.ppermute(
+                latest, axis_name=row_axis, perm=[(nth, nth ^ rr) for nth in range(state_now)]
+            )
+        )
+        rr = rr + 1
+    current_arr = jnp.stack(runs, 0)[u_next ^ jnp.arange(state_now)]
+    seen_now = reach_meshes_all(current_arr, vector)
+    return seen_now
+
+
+time_the_units = functools.partial(plan_racks_on, vector=3, row_axis="chan", message=2)
 
 
 def phase_pair(products, modulus):
@@ -145,7 +182,7 @@
     predicted = predict(own_cuts, subgrid_stations, station_beams, visibility_uv)
     chan_count = lax.axis_size("chan")
     outgoing = predicted.reshape(2, SUB_TILE // chan_count, chan_count, predicted.shape[2])
-    regrouped = lax.all_to_all(outgoing, "chan", split_axis=2, concat_axis=3, tiled=True)
+    regrouped = time_the_units(outgoing)
     total_rows = regrouped.shape[3]
     time_step = jnp.mod(jnp.arange(total_rows, dtype=jnp.int32), TIMES)
     live_mask = time_step[None, None, :] < live_counts[:, :, None]

time: 119 us -> 117 us (0.983)
  starting transfers between devices: 3.3 us -> 1.96 us
  other arithmetic: 43 us -> 44.3 us
    all_to_all x1 -> x0, waiting for transfers between devices: 3.74 us -> none  [on_device(): lax.all_to_all(outgoing, 'chan', split_axis=2, concat_axis=3, tiled=True)]
    all_to_all x1 -> x0, starting transfers between devices: 3.25 us -> none  [on_device(): lax.all_to_all(outgoing, 'chan', split_axis=2, concat_axis=3, tiled=True)]
    ppermute x0 -> x3, waiting for transfers between devices: none -> 2.7 us  [plan_racks_on(): jax.lax.ppermute(latest, axis_name=row_axis, perm=[(nth, nth ^ rr) for nt...]
    ppermute x0 -> x3, starting transfers between devices: none -> 1.92 us  [plan_racks_on(): jax.lax.ppermute(latest, axis_name=row_axis, perm=[(nth, nth ^ rr) for nt...]
    another operation x1 -> x2, other arithmetic: 35.5 us -> 35.5 us
  transfers between devices with their start and end apart: 3 -> 5, of which waited for: 2 -> 3; matrix products, arithmetic and copies ran while one was open for 38% -> 39% of each run, Pallas kernels for 0% -> 0%
where the time goes in v1:
time: 117 us
  other arithmetic  44.3 us (38%)
  matrix products  33.7 us (29%)
  waiting for transfers between devices  18 us (15%)
  between operations  13.7 us (12%)
  local copies, waits for them, and re-layouts  5.5 us (5%)
  starting transfers between devices  1.96 us (2%)
    another operation x1, other arithmetic  35.5 us
    dot_general x4, matrix products, narrow_mix(): return jnp.einsum(pattern, left, right, preferred_element_type=jnp.float32)  16.4 us
    reduce_scatter x1, waiting for transfers between devices, on_device(): lax.psum_scatter(group_cuts, 'tile', scatter_dimension=0, tiled=True)  14.6 us
    dot_general x12, matrix products, exact_mix(): return jnp.einsum(pattern, left, right, precision=lax.Precision.HIGHEST)  11.4 us
    another operation x1, other arithmetic, tile_cuts(): jnp.stack([ev_real, ev_imag], axis=1).reshape(columns, 2 * block_size * SG)  6.18 us
    dot_general x1, matrix products, tile_cuts(): jnp.dot(strip_rows, phase_table, preferred_element_type=jnp.float32)  6 us
    ppermute x3, waiting for transfers between devices, plan_racks_on(): jax.lax.ppermute(latest, axis_name=row_axis, perm=[(nth, nth ^ rr) for nt...  2.7 us
  transfers between devices with their start and end apart: 5, of which 3 were waited for; matrix products, arithmetic and copies ran while one was open for 39% of the time, Pallas kernels for 0%

profile of v1, /device:TPU:0, one launch (start us, length us, event | category | flops | bytes accessed | tf_op | source)
XLA Modules:
  0.0 117.1 jit_solution(6607002912501205430)
XLA Ops:
  6.5 0.7 all-gather.2.cloned.1.call-update
  7.3 0.8 fusion.81
  8.3 0.8 fusion.82
  9.1 0.7 gather_fusion
  9.9 0.7 gather_fusion.1
  10.6 0.7 broadcast_compare_fusion
  11.7 35.5 %cosine_convert_fusion = (bf16[2048,1,32,32]{0,3,2,1:T(8,128)(2,1)S(1)}, bf16[2048,1,32,32]{0,3,2,1:T(8,128)(2,1)}) fusion(s32[32,32]{1,0:T(8,128)S(1)} %iota_add_fusion, s32[2048]{0:T(1024)S(1)} %iota_add_fusion.2), kind=kLoop, calls=%fused_computation.13 | loop fusion | flops 35651584 | bytes 8400896 | tf_op jit(solution)/shard_map/convert
  47.2 6.2 %pad_maximum_fusion = bf16[2048,2,32,32]{0,3,2,1:T(8,128)(2,1)} fusion(bf16[2048,1,32,32]{0,3,2,1:T(8,128)(2,1)} %get-tuple-element.31, bf16[2048,1,32,32]{0,3,2,1:T(8,128)(2,1)S(1)} %get-tuple-element.30), kind=kLoop, calls=%fused_computation.11 | loop fusion | flops 4194304 | bytes 16777216 | tf_op jit(solution)/shard_map/while/body/eval_jaxpr/stack | solution.py:74
  53.4 6.0 %convolution_convert_fusion = bf16[2048,256]{1,0:T(8,128)(2,1)S(1)} fusion(bf16[2048,2048]{0,1:T(8,128)(2,1)} %bitcast.105, bf16[256,2048]{1,0:T(8,128)(2,1)} %bitcast.120), kind=kOutput, calls=%fused_computation.14 | convolution fusion | flops 2148007936 | bytes 10485760 | tf_op jit(solution)/shard_map/while/body/eval_jaxpr/dot_general | solution.py:78
  59.4 4.0 %fusion.15 = f32[32,32,32]{2,1,0:T(8,128)S(1)} fusion(s32[256]{0:T(256)S(1)} %sub.67, s32[32,32]{1,0:T(8,128)S(1)} %iota_add_fusion.1, bf16[256,2,32,32]{0,3,2,1:T(8,128)(2,1)S(1)} %bitcast.121), kind=kOutput, calls=%fused_computation.45 | convolution fusion | flops 20709376 | bytes 672768 | tf_op jit(solution)/shard_map/while/body/eval_jaxpr/jal,ljb->jab/dot_general | solution.py:59
  63.4 4.0 %fusion.14 = f32[32,32,32]{2,1,0:T(8,128)S(1)} fusion(s32[256]{0:T(256)S(1)} %sub.67, s32[32,32]{1,0:T(8,128)S(1)} %iota_add_fusion.1, bf16[256,2,32,32]{0,3,2,1:T(8,128)(2,1)S(1)} %bitcast.122), kind=kOutput, calls=%fused_computation.44 | convolution fusion | flops 20709376 | bytes 672768 | tf_op jit(solution)/shard_map/while/body/eval_jaxpr/jal,ljb->jab/dot_general | solution.py:59
  67.4 4.3 %fusion.4 = f32[32,1,32,32]{3,2,0,1:T(8,128)S(1)} fusion(f32[32,32,32]{2,1,0:T(8,128)S(1)} %fusion.15, s32[256]{0:T(256)S(1)} %sub.67, s32[32,32]{1,0:T(8,128)S(1)} %iota_add_fusion.1, bf16[256,2,32,32]{0,3,2,1:T(8,128)(2,1)S(1)} %bitcast.123), kind=kOutput, calls=%fused_computation.23 | convolution fusion | flops 21004288 | bytes 1197056 | tf_op jit(solution)/shard_map/while/body/eval_jaxpr/jal,ljb->jab/dot_general | solution.py:59
  71.7 4.1 %fusion.3 = f32[32,1,32,32]{3,2,0,1:T(8,128)S(1)} fusion(f32[32,32,32]{2,1,0:T(8,128)S(1)} %fusion.14, s32[256]{0:T(256)S(1)} %sub.67, s32[32,32]{1,0:T(8,128)S(1)} %iota_add_fusion.1, bf16[256,2,32,32]{0,3,2,1:T(8,128)(2,1)S(1)} %bitcast.124), kind=kOutput, calls=%fused_computation.21 | convolution fusion | flops 21004288 | bytes 1197056 | tf_op jit(solution)/shard_map/while/body/eval_jaxpr/jal,ljb->jab/dot_general | solution.py:59
  76.0 1.2 %reshape.300 = f32[32,2048]{1,0:T(8,128)} reshape(f32[32,2,32,32]{3,2,1,0:T(8,128)S(1)} %copy.19) | data formatting | bytes 524288 | tf_op jit(solution)/shard_map/reshape | solution.py:105
  77.3 14.6 %reduce-scatter.2.cloned.1.call-done = f32[16,2048]{1,0:T(8,128)} async-done(((f32[32,2048]{1,0:T(8,128)}), f32[16,2048]{1,0:T(8,128)}) %reduce-scatter.2.cloned.1.call-update) | async-done | bytes 131088 | tf_op jit(solution)/shard_map/reduce_scatter | solution.py:181
  91.8 1.1 reshape.301
  92.9 0.6 fusion.23
  93.5 0.6 fusion.22
  94.1 0.6 fusion.10
  94.7 0.6 fusion.46
  95.3 0.6 fusion.39
  95.9 0.6 fusion.9
  96.5 0.9 fusion.8
  97.4 0.6 multiply_add_fusion
  98.0 1.3 %fusion.20 = f32[16,32,128]{2,1,0:T(8,128)S(1)} fusion(f32[16,32,32]{2,1,0:T(8,128)S(1)} %get-tuple-element.27, f32[16,128]{1,0:T(8,128)S(1)} %get-tuple-element.37, f32[32]{0:T(128)S(1)} %iota_convert_fusion), kind=kOutput, calls=%fused_computation.58 | convolution fusion | flops 25362432 | bytes 336000 | tf_op jit(solution)/shard_map/jxy,jky->jxk/dot_general | solution.py:63
  99.3 1.3 %fusion.18 = f32[16,32,128]{2,1,0:T(8,128)S(1)} fusion(f32[16,32,32]{2,1,0:T(8,128)S(1)} %get-tuple-element.27, f32[16,128]{1,0:T(8,128)S(1)} %get-tuple-element.37, f32[32]{0:T(128)S(1)} %iota_convert_fusion), kind=kOutput, calls=%fused_computation.57 | convolution fusion | flops 25296896 | bytes 336000 | tf_op jit(solution)/shard_map/jxy,jky->jxk/dot_general | solution.py:63
  100.6 1.3 %fusion.5 = f32[16,128,32]{1,2,0:T(8,128)S(1)} fusion(f32[16,32,128]{2,1,0:T(8,128)S(1)} %fusion.20, f32[16,32,32]{2,1,0:T(8,128)S(1)} %get-tuple-element.26, f32[16,128]{1,0:T(8,128)S(1)} %get-tuple-element.37, f32[32]{0:T(128)S(1)} %iota_convert_fusion), kind=kOutput, calls=%fused_computation.25 | convolution fusion | flops 25362432 | bytes 598144 | tf_op jit(solution)/shard_map/jxy,jky->jxk/dot_general | solution.py:63
  102.0 2.4 %multiply_reduce_fusion = (f32[16,128]{1,0:T(8,128)S(1)}, f32[16,128]{1,0:T(8,128)S(1)}, f32[16,128]{1,0:T(8,128)S(1)}, f32[16,128]{1,0:T(8,128)S(1)}) fusion(f32[32]{0:T(128)S(1)} %iota_convert_fusion, f32[16,128]{1,0:T(8,128)S(1)} %get-tuple-element.36, f32[16,128,32]{1,2,0:T(8,128)S(1)} %fusion.5, f32[16,32,128]{2,1,0:T(8,128)S(1)} %fusion.18, ...), kind=kOutput, calls=%fused_computation.48 | convolution fusion | flops 26140672 | bytes 639104 | tf_op jit(solution)/shard_map/jxy,jky->jxk/dot_general | solution.py:63
  104.5 1.5 %collective-permute-start.1 = (f32[2,4,1,128]{3,1,0,2:T(4,128)S(1)}, f32[2,4,1,128]{3,1,0,2:T(4,128)S(1)}, u32[]{:S(2)}, u32[]{:S(2)}) collective-permute-start(f32[2,4,1,128]{3,1,0,2:T(4,128)S(1)} %bitcast.114), channel_id=1, source_target_pairs={{0,4},{2,6},{4,0},{6,2},{1,5},{3,7},{5,1},{7,3},{8,12},{10,14},{12... | collective-permute-start | bytes 12296 | tf_op jit(solution)/shard_map/ppermute | solution.py:40
  106.3 1.8 %collective-permute-done.1 = f32[2,4,1,128]{3,1,0,2:T(4,128)S(1)} collective-permute-done((f32[2,4,1,128]{3,1,0,2:T(4,128)S(1)}, f32[2,4,1,128]{3,1,0,2:T(4,128)S(1)}, u32[]{:S(2)}, u32[]{:S(2)}) %collective-permute-start.1) | collective-permute-done | bytes 4128 | tf_op jit(solution)/shard_map/ppermute | solution.py:40
  108.2 0.9 collective-permute-done.2
  109.6 0.6 broadcast_select_fusion
  (39 shorter events, 2.0 us)
Async XLA Ops:
  6.5 2.6 %copy-start = (f32[2,64,1024]{2,1,0:T(8,128)S(1)}, f32[2,64,1024]{2,1,0:T(8,128)}, u32[]{:S(2)}) copy-start(f32[2,64,1024]{2,1,0:T(8,128)} %param.8) | copy-start | bytes 1572868
  6.5 46.8 %all-gather.2.cloned.1.call-start = ((), (), s32[]{:S(2)}) async-start(), calls=%async_computation.1 | async-start | bytes 1310720 | tf_op jit(solution)/shard_map/all_gather | solution.py:174
  7.3 84.6 %reduce-scatter.2.cloned.1.call-start = ((), (), s32[]{:S(2)}) async-start(), calls=%async_computation.2 | async-start | bytes 393216 | tf_op jit(solution)/shard_map/reduce_scatter | solution.py:181
  67.4 9.9 %copy-start.2 = (f32[2,16,128]{2,1,0:T(8,128)S(1)}, f32[2,16,128]{2,1,0:T(8,128)}, u32[]{:S(2)}) copy-start(f32[2,16,128]{2,1,0:T(8,128)} %param.11) | copy-start | bytes 49156
  75.8 33.9 %copy-start.1 = (f32[2,4,1,512]{3,2,1,0:T(1,128)S(1)}, f32[2,4,1,512]{3,2,1,0:T(1,128)}, u32[]{:S(2)}) copy-start(f32[2,4,1,512]{3,2,1,0:T(1,128)} %param.12) | copy-start | bytes 49156
  104.4 1.9 %collective-permute-start = (f32[2,4,1,128]{3,1,0,2:T(4,128)S(1)}, f32[2,4,1,128]{3,1,0,2:T(4,128)S(1)}, u32[]{:S(2)}, u32[]{:S(2)}) collective-permute-start(f32[2,4,1,128]{3,1,0,2:T(4,128)S(1)} %bitcast.115), channel_id=1, source_target_pairs={{0,2},{2,0},{4,6},{6,4},{1,3},{3,1},{5,7},{7,5},{8,10},{10,8},{12,... | collective-permute-start | bytes 12296 | tf_op jit(solution)/shard_map/ppermute | solution.py:40
  104.5 3.7 %collective-permute-start.1 = (f32[2,4,1,128]{3,1,0,2:T(4,128)S(1)}, f32[2,4,1,128]{3,1,0,2:T(4,128)S(1)}, u32[]{:S(2)}, u32[]{:S(2)}) collective-permute-start(f32[2,4,1,128]{3,1,0,2:T(4,128)S(1)} %bitcast.114), channel_id=1, source_target_pairs={{0,4},{2,6},{4,0},{6,2},{1,5},{3,7},{5,1},{7,3},{8,12},{10,14},{12... | collective-permute-start | bytes 12296 | tf_op jit(solution)/shard_map/ppermute | solution.py:40
  106.0 3.0 %collective-permute-start.2 = (f32[2,4,1,128]{3,1,0,2:T(4,128)S(1)}, f32[2,4,1,128]{3,1,0,2:T(4,128)S(1)}, u32[]{:S(2)}, u32[]{:S(2)}) collective-permute-start(f32[2,4,1,128]{3,1,0,2:T(4,128)S(1)} %bitcast.113), channel_id=1, source_target_pairs={{0,6},{2,4},{4,2},{6,0},{1,7},{3,5},{5,3},{7,1},{8,14},{10,12},{12... | collective-permute-start | bytes 12296 | tf_op jit(solution)/shard_map/ppermute | solution.py:40
Sparse Core Ops, SparseCore 0:
  8.9 30.8 all-gather.1
  77.3 14.4 reduce-scatter.1
